TPU v7x, 128 devices: a whole 4x4x4 slice. The times are simulated.
128 devices in a mesh: dp: 16 (over z, y), tp: 8 (over x, core).
Axes of the slice: x: 4, y: 4, z: 4, core: 2. Of those that a mesh axis runs over, the one named last changes fastest.
Arguments:
- w_up: bfloat16 [2, 1536, 6144], P(None, None, 'tp')
- w_down: bfloat16 [2, 6144, 1536], P(None, 'tp')
- x_saved: bfloat16 [2, 16, 2048, 1536], P(None, 'dp')
- h_saved: bfloat16 [2, 16, 2048, 6144], P(None, 'dp', None, 'tp')
- grad_out: bfloat16 [16, 2048, 1536], P('dp')
Outputs:
- output 1: bfloat16 [16, 2048, 1536], P('dp')
- output 2: float32 [2, 1536, 6144], P(None, None, 'tp')
- output 3: float32 [2, 6144, 1536], P(None, 'tp')
All inputs are finite; a program needn't handle non-finite values.
Results may differ from a plain program's by a relative error of at most 0.0137507.
Values are sent between devices in bfloat16 or wider.
A program may use at most 1 GiB of HBM per device.

v0:
```python
import jax
import jax.numpy as jnp
from jax import lax
from jax.sharding import PartitionSpec as P


def gelu_parts(hidden):
    tanh_val = jnp.tanh(0.7978845608028654 * (hidden + 0.044715 * hidden * hidden * hidden))
    gelu_out = 0.5 * hidden * (1.0 + tanh_val)
    gelu_slope = 0.5 * (1.0 + tanh_val) + 0.5 * hidden * (1.0 - tanh_val * tanh_val) * 0.7978845608028654 * (1.0 + 0.134145 * hidden * hidden)
    return gelu_out, gelu_slope


def solution(mesh):
    def run_backward(w_up, w_down, x_saved, h_saved, grad_out):
        layer_count = w_up.shape[0]
        grad_cur = grad_out
        up_grads = {}
        down_grads = {}
        for layer_idx in reversed(range(layer_count)):
            gelu_out, gelu_slope = gelu_parts(h_saved[layer_idx].astype(jnp.float32))
            act_grad = jnp.einsum("bsd,fd->bsf", grad_cur, w_down[layer_idx], preferred_element_type=jnp.float32)
            hid_grad = (act_grad * gelu_slope).astype(jnp.bfloat16)
            part_sum = jnp.einsum("bsf,df->bsd", hid_grad, w_up[layer_idx], preferred_element_type=jnp.float32).astype(jnp.bfloat16)
            full_sum = lax.psum(part_sum, "tp")
            down_grads[layer_idx] = jnp.einsum("bsf,bsd->fd", gelu_out.astype(jnp.bfloat16), grad_cur, preferred_element_type=jnp.float32)
            up_grads[layer_idx] = jnp.einsum("bsd,bsf->df", x_saved[layer_idx], hid_grad, preferred_element_type=jnp.float32)
            grad_cur = (grad_cur.astype(jnp.float32) + full_sum.astype(jnp.float32)).astype(jnp.bfloat16)
        up_total = lax.psum(jnp.stack([up_grads[layer_idx] for layer_idx in range(layer_count)]), "dp")
        down_total = lax.psum(jnp.stack([down_grads[layer_idx] for layer_idx in range(layer_count)]), "dp")
        return grad_cur, up_total, down_total
    return jax.shard_map(run_backward, mesh=mesh, in_specs=(P(None, None, "tp"), P(None, "tp", None), P(None, "dp", None, None), P(None, "dp", None, "tp"), P("dp", None, None)), out_specs=(P("dp", None, None), P(None, None, "tp"), P(None, "tp", None)), check_vma=False)
```

profile of v0, /device:TPU:0, one launch (start us, length us, event | category | flops | bytes accessed | tf_op | source)
XLA Modules:
  0.0 488.5 jit_solution(9220252319749229417)
XLA Ops:
  7.2 0.0 all-reduce.5.cloned.1.call-start
  7.2 0.0 copy-start
  7.2 11.1 %fusion.23 = bf16[2048,768]{1,0:T(8,128)(2,1)S(1)} fusion(bf16[1,2048,1536]{2,1,0:T(8,128)(2,1)} %param.9, bf16[2,1,2048,768]{3,2,1,0:T(8,128)(2,1)} %param.8, bf16[2,768,1536]{2,1,0:T(8,128)(2,1)} %param.6), kind=kOutput, calls=%fused_computation.41 | convolution fusion | flops 4863295488 | bytes 14942208 | tf_op jit(solution)/shard_map/bsd,fd->bsf/dot_general | solution.py:22
  18.4 7.0 %fusion.14 = bf16[1,2048,1536]{2,1,0:T(8,128)(2,1)} fusion(bf16[2048,768]{1,0:T(8,128)(2,1)S(1)} %fusion.23, bf16[2,1536,768]{2,1,0:T(8,128)(2,1)S(1)} %copy-done), kind=kOutput, calls=%fused_computation.32 | convolution fusion | flops 4834983936 | bytes 11796480 | tf_op jit(solution)/shard_map/bsf,df->bsd/dot_general | solution.py:24
  25.4 0.0 all-reduce.5.cloned.1.call-update
  25.4 0.2 all-reduce.7.cloned.1.call-start
  25.7 9.5 %fusion.67 = f32[1,1536,768]{1,2,0:T(8,128)} fusion(bf16[2048,768]{1,0:T(8,128)(2,1)S(1)} %fusion.23, bf16[2,1,2048,1536]{3,2,1,0:T(8,128)(2,1)} %param.7), kind=kOutput, calls=%fused_computation.79 | convolution fusion | flops 4831838208 | bytes 14155776 | tf_op jit(solution)/shard_map/bsd,bsf->df/dot_general | solution.py:27
  35.2 10.1 %fusion.58 = f32[1,768,1536]{2,1,0:T(8,128)} fusion(bf16[1,2048,1536]{2,1,0:T(8,128)(2,1)} %param.9, bf16[2,1,2048,768]{3,2,1,0:T(8,128)(2,1)} %param.8), kind=kOutput, calls=%fused_computation.76 | convolution fusion | flops 4847566848 | bytes 14155776 | tf_op jit(solution)/shard_map/bsf,bsd->fd/dot_general | solution.py:26
  45.3 66.9 %all-reduce.5.cloned.1.call-done = bf16[1,2048,1536]{2,1,0:T(8,128)(2,1)} async-done(((bf16[1,2048,1536]{2,1,0:T(8,128)(2,1)}), bf16[1,2048,1536]{2,1,0:T(8,128)(2,1)}) %all-reduce.5.cloned.1.call-update) | async-done | bytes 6291472 | tf_op jit(solution)/shard_map/psum | solution.py:25
  112.2 14.0 %fusion.37 = bf16[2048,768]{1,0:T(8,128)(2,1)S(1)} fusion(bf16[2,1,2048,768]{3,2,1,0:T(8,128)(2,1)} %param.8, bf16[2,768,1536]{2,1,0:T(8,128)(2,1)} %param.6, bf16[1,2048,1536]{2,1,0:T(8,128)(2,1)} %all-reduce.5.cloned.1.call-done, bf16[1,2048,1536]{2,1,0:T(8,128)(2,1)} %param.9), kind=kOutput, calls=%fused_computation.55 | convolution fusion | flops 4875878400 | bytes 21233664 | tf_op jit(solution)/shard_map/bsd,fd->bsf/dot_general | solution.py:22
  126.2 8.6 %fusion.15 = bf16[1,2048,1536]{2,1,0:T(8,128)(2,1)} fusion(bf16[2048,768]{1,0:T(8,128)(2,1)S(1)} %fusion.37, bf16[2,1536,768]{2,1,0:T(8,128)(2,1)} %param.5), kind=kOutput, calls=%fused_computation.33 | convolution fusion | flops 4834983936 | bytes 11796480 | tf_op jit(solution)/shard_map/bsf,df->bsd/dot_general | solution.py:24
  134.8 0.0 all-reduce.7.cloned.1.call-update
  134.8 0.3 all-reduce.9.cloned.1.call-start
  135.1 7.3 %fusion.64 = f32[1,1536,768]{1,2,0:T(8,128)S(1)} fusion(bf16[2048,768]{1,0:T(8,128)(2,1)S(1)} %fusion.37, bf16[2,1,2048,1536]{3,2,1,0:T(8,128)(2,1)} %param.7), kind=kOutput, calls=%fused_computation.78 | convolution fusion | flops 4831838208 | bytes 14155776 | tf_op jit(solution)/shard_map/bsd,bsf->df/dot_general | solution.py:27
  142.5 0.0 slice-start
  142.5 7.1 %pad_maximum_fusion = f32[2,1536,768]{1,2,0:T(8,128)} fusion(f32[1,1536,768]{1,2,0:T(8,128)} %fusion.67, f32[1,1536,768]{1,2,0:T(8,128)S(1)} %fusion.64), kind=kLoop, calls=%fused_computation.28 | loop fusion | flops 2359296 | bytes 18874368 | tf_op jit(solution)/shard_map/stack | solution.py:29
  149.5 12.0 %fusion.61 = f32[1,768,1536]{2,1,0:T(8,128)S(1)} fusion(bf16[2,1,2048,768]{3,2,1,0:T(8,128)(2,1)} %param.8, bf16[1,2048,1536]{2,1,0:T(8,128)(2,1)} %all-reduce.5.cloned.1.call-done, bf16[1,2048,1536]{2,1,0:T(8,128)(2,1)} %param.9), kind=kOutput, calls=%fused_computation.77 | convolution fusion | flops 4860149760 | bytes 20447232 | tf_op jit(solution)/shard_map/bsf,bsd->fd/dot_general | solution.py:26
  161.5 4.6 pad_maximum_fusion.1
  166.1 0.0 all-reduce.9.cloned.1.call-update
  166.2 52.8 %all-reduce.7.cloned.1.call-done = bf16[1,2048,1536]{2,1,0:T(8,128)(2,1)} async-done(((bf16[1,2048,1536]{2,1,0:T(8,128)(2,1)}), bf16[1,2048,1536]{2,1,0:T(8,128)(2,1)}) %all-reduce.7.cloned.1.call-update) | async-done | bytes 6291472 | tf_op jit(solution)/shard_map/psum | solution.py:25
  218.9 11.6 %add_convert_fusion = bf16[1,2048,1536]{2,1,0:T(8,128)(2,1)} fusion(bf16[1,2048,1536]{2,1,0:T(8,128)(2,1)} %all-reduce.7.cloned.1.call-done, bf16[1,2048,1536]{2,1,0:T(8,128)(2,1)} %all-reduce.5.cloned.1.call-done, bf16[1,2048,1536]{2,1,0:T(8,128)(2,1)} %param.9), kind=kLoop, calls=%fused_computation.26 | loop fusion | flops 25165824 | bytes 25165824 | tf_op jit(solution)/shard_map/convert_element_type | solution.py:28
  230.6 233.6 %all-reduce.9.cloned.1.call-done = (f32[2,1536,768]{1,2,0:T(8,128)}, f32[2,768,1536]{2,1,0:T(8,128)}) async-done(((f32[2,1536,768]{1,2,0:T(8,128)}, f32[2,768,1536]{2,1,0:T(8,128)}), (f32[2,1536,768]{1,2,0:T(8,128)}, f32[2,768,1536]{2,1,0:T(8,128)})) %all-reduce.9.cloned.1.call-update) | async-done | bytes 18874384 | tf_op jit(solution)/shard_map/psum | solution.py:29
  464.2 9.6 %copy.8 = f32[2,1536,768]{2,1,0:T(8,128)} copy(f32[2,1536,768]{1,2,0:T(8,128)} %get-tuple-element.6) | data formatting | bytes 18874368
  473.7 8.3 %copy.13 = f32[2,768,1536]{2,1,0:T(8,128)} copy(f32[2,768,1536]{2,1,0:T(8,128)} %get-tuple-element.10) | data formatting | bytes 18874368
  (5 shorter events, 0.0 us)
Async XLA Ops:
  7.2 105.0 %all-reduce.5.cloned.1.call-start = ((), (), s32[]{:S(2)}) async-start(), calls=%async_computation | async-start | bytes 12582912 | tf_op jit(solution)/shard_map/psum | solution.py:25
  7.2 11.2 %copy-start = (bf16[2,1536,768]{2,1,0:T(8,128)(2,1)S(1)}, bf16[2,1536,768]{2,1,0:T(8,128)(2,1)}, u32[]{:S(2)}) copy-start(bf16[2,1536,768]{2,1,0:T(8,128)(2,1)} %param.5) | copy-start | bytes 14155780
  25.4 193.5 %all-reduce.7.cloned.1.call-start = ((), (), s32[]{:S(2)}) async-start(), calls=%async_computation.1 | async-start | bytes 12582912 | tf_op jit(solution)/shard_map/psum | solution.py:25
  134.8 329.3 %all-reduce.9.cloned.1.call-start = ((), (), s32[]{:S(2)}) async-start(), calls=%async_computation.2 | async-start | bytes 37748736 | tf_op jit(solution)/shard_map/psum | solution.py:29
  142.5 19.1 %slice-start = ((s8[4718592]{0:T(1024)(128)(4,1)}), s8[4194304]{0:T(1024)(128)(4,1)S(1)}, s32[]{:S(2)}) async-start(s8[4718592]{0:T(1024)(128)(4,1)} %bitcast.158), calls=%async_computation.3 | async-start | bytes 8388608
  149.5 12.0 %slice-start.1 = ((s8[4718592]{0:T(1024)(128)(4,1)}), s8[524288]{0:T(1024)(128)(4,1)S(1)}, s32[]{:S(2)}) async-start(s8[4718592]{0:T(1024)(128)(4,1)} %bitcast.158), calls=%async_computation.4 | async-start | bytes 1048576
Sparse Core Ops, SparseCore 0:
  25.6 86.5 all-reduce.4
  135.0 83.9 all-reduce.6
  223.4 240.7 all-reduce.8
where the time goes:
time: 489 us
  waiting for transfers between devices  353 us (72%)
  matrix products  79.7 us (16%)
  other arithmetic  23.3 us (5%)
  local copies, waits for them, and re-layouts  17.9 us (4%)
  between operations  13.8 us (3%)
    psum x1, waiting for transfers between devices, run_backward(): lax.psum(jnp.stack([up_grads[layer_idx] for layer_idx in range(layer_coun...  234 us
    psum x2, waiting for transfers between devices, run_backward(): full_sum = lax.psum(part_sum, 'tp')  120 us
    dot_general x2, matrix products, run_backward(): jnp.einsum('bsd,fd->bsf', grad_cur, w_down[layer_idx], preferred_element_...  25.1 us
    dot_general x2, matrix products, run_backward(): jnp.einsum('bsf,bsd->fd', gelu_out.astype(jnp.bfloat16), grad_cur, prefer...  22.1 us
    unnamed x8, local copies, waits for them, and re-layouts  17.9 us
    dot_general x2, matrix products, run_backward(): jnp.einsum('bsd,bsf->df', x_saved[layer_idx], hid_grad, preferred_element...  16.8 us
    dot_general x2, matrix products, run_backward(): jnp.einsum('bsf,df->bsd', hid_grad, w_up[layer_idx], preferred_element_ty...  15.7 us
    convert_element_type x1, other arithmetic, run_backward(): (grad_cur.astype(jnp.float32) + full_sum.astype(jnp.float32)).astype(jnp....  11.6 us
  transfers between devices with their start and end apart: 3, of which 3 were waited for; matrix products, arithmetic and copies ran while one was open for 13% of the time, Pallas kernels for 0%

commit v1 on v0

v1 whole, which is shorter than its diff:
```python
import jax
import jax.numpy as jnp
from jax import lax
from jax.experimental import pallas as pl
from jax.experimental.pallas import tpu as pltpu
from jax.sharding import PartitionSpec as P

MESH = pl.DeviceIdType.MESH
F32, BF16 = jnp.float32, jnp.bfloat16
T, D, F = 2048, 1536, 768
HALF = T // 2
TOK = HALF // 4
N1, N2 = F // 8, F // 32
RS1, RS2, AG2, AG1 = range(4)
DIRS = ((0, 1), (1, -1))


def gelu_parts(hidden):
    tanh_val = jnp.tanh(0.7978845608028654 * (hidden + 0.044715 * hidden * hidden * hidden))
    gelu_out = 0.5 * hidden * (1.0 + tanh_val)
    gelu_slope = 0.5 * (1.0 + tanh_val) + 0.5 * hidden * (1.0 - tanh_val * tanh_val) * 0.7978845608028654 * (1.0 + 0.134145 * hidden * hidden)
    return gelu_out, gelu_slope


def backward_kernel(wu_hbm, wd_hbm, x_hbm, h_hbm, g_hbm, buf_a, w0, w1, w2, w3,
                    buf_b, pair_in, h_buf, dh_buf, wu_buf, wd_buf, x_tile, ring1, ring2, xring,
                    dp_send, dp_recv, dp_free, x_send, x_recv, x_free, pair_send, pair_recv, pair_free, load_sem, x_sem):
    weight_sums = (w0, w1, w2, w3)
    dp_pos, tp_pos = lax.axis_index("dp"), lax.axis_index("tp")
    core = lax.rem(tp_pos, 2)
    pos = {"x": tp_pos // 2, "y": lax.rem(dp_pos, 4), "z": dp_pos // 4}

    def wrap(value):
        return lax.rem(value + 4, 4)

    def neighbour(axis, step):
        moved = wrap(pos[axis] + step)
        if axis == "x":
            return {"dp": dp_pos, "tp": moved * 2 + core}
        if axis == "y":
            return {"dp": pos["z"] * 4 + moved, "tp": tp_pos}
        return {"dp": moved * 4 + pos["y"], "tp": tp_pos}

    partner = {"dp": dp_pos, "tp": pos["x"] * 2 + 1 - core}

    def load(src, dst, k):
        copy = pltpu.make_async_copy(src, dst, load_sem.at[k])
        copy.start()
        return copy

    load_h = load(h_hbm.at[1, 0], h_buf, 0)
    load_g = load(g_hbm.at[0], buf_a, 1)
    load_wd = load(wd_hbm.at[1], wd_buf, 2)
    load_wu = load(wu_hbm.at[1], wu_buf, 3)

    barrier = pltpu.get_barrier_semaphore()
    for axis in "xyz":
        for _, step in DIRS:
            pl.semaphore_signal(barrier, inc=1, device_id=neighbour(axis, step), device_id_type=MESH)
    pl.semaphore_signal(barrier, inc=1, device_id=partner, device_id_type=MESH)

    copies = {}

    def dp_start(m, stage, colour, di, piece, src, dst, axis):
        k = ((stage * 2 + colour) * 2 + di) * 3 + piece
        copy = pltpu.make_async_remote_copy(src_ref=src, dst_ref=dst, send_sem=dp_send.at[m, k], recv_sem=dp_recv.at[m, k],
                                            device_id=neighbour(axis, DIRS[di][1]), device_id_type=MESH)
        copy.start()
        copies[m, stage, colour, di, piece] = copy

    def level(m, stage, colour):
        first, second = ("y", "z") if colour == 0 else ("z", "y")
        base = colour * (F // 2)
        if stage in (RS1, AG1):
            return first, base, N1, ring1.at[m % 2, colour]
        return second, base + pos[first] * N1, N2, ring2.at[m % 2, colour]

    def rows(base, j, n):
        return pl.ds(pl.multiple_of(base + j * n, 8), n)

    def rs_start(m, stage):
        w = weight_sums[m]
        for piece in range(2):
            for colour in range(2):
                axis, base, n, ring = level(m, stage, colour)
                for di, step in DIRS:
                    if piece == 0:
                        src = w.at[di, rows(base, wrap(pos[axis] + 2), n)]
                    else:
                        src = w.at[1 - di, rows(base, wrap(pos[axis] + step), n)]
                    dp_start(m, stage, colour, di, piece, src, ring.at[di, piece], axis)

    def rs_mid(m, stage):
        w = weight_sums[m]
        for colour in range(2):
            axis, base, n, ring = level(m, stage, colour)
            for di, step in DIRS:
                copies[m, stage, colour, di, 0].wait_recv()
                near = rows(base, wrap(pos[axis] + step), n)
                w[di, near, :] = w[di, near, :] + ring[di, 0]
                dp_start(m, stage, colour, di, 2, w.at[di, near], ring.at[di, 2], axis)

    def rs_end(m, stage):
        w = weight_sums[m]
        for colour in range(2):
            axis, base, n, ring = level(m, stage, colour)
            for di, _ in DIRS:
                copies[m, stage, colour, di, 1].wait_recv()
                copies[m, stage, colour, di, 2].wait_recv()
            own = rows(base, pos[axis], n)
            for di, _ in DIRS:
                w[di, own, :] = w[di, own, :] + ring[di, 2] + ring[1 - di, 1]
            for di, step in DIRS:
                for piece in range(3):
                    copies[m, stage, colour, di, piece].wait_send()
            for di, step in DIRS:
                pl.semaphore_signal(dp_free.at[m, stage, colour, di], inc=1, device_id=neighbour(axis, -step), device_id_type=MESH)

    def ag_start(m, stage):
        w = weight_sums[m]
        for piece in range(2):
            for colour in range(2):
                axis, base, n, _ = level(m, stage, colour)
                own = rows(base, pos[axis], n)
                for di, _ in DIRS:
                    if piece == 0:
                        pl.semaphore_wait(dp_free.at[m, RS2 if stage == AG2 else RS1, colour, di], 1)
                    part = w.at[di if piece == 0 else 1 - di, own]
                    dp_start(m, stage, colour, di, piece, part, part, axis)

    def ag_mid(m, stage):
        w = weight_sums[m]
        for colour in range(2):
            axis, base, n, _ = level(m, stage, colour)
            for di, step in DIRS:
                copies[m, stage, colour, di, 0].wait_recv()
                part = w.at[di, rows(base, wrap(pos[axis] - step), n)]
                dp_start(m, stage, colour, di, 2, part, part, axis)

    def ag_end(m, stage):
        for colour in range(2):
            for di, _ in DIRS:
                copies[m, stage, colour, di, 1].wait_recv()
                copies[m, stage, colour, di, 2].wait_recv()

    def dp_step(m, k):
        if k == 0:
            rs_start(m, RS1)
        elif k == 1:
            rs_mid(m, RS1)
        elif k == 2:
            rs_end(m, RS1)
            rs_start(m, RS2)
        elif k == 3:
            rs_mid(m, RS2)
        elif k == 4:
            rs_end(m, RS2)
            ag_start(m, AG2)
        elif k == 5:
            ag_mid(m, AG2)
        elif k == 6:
            ag_end(m, AG2)
            ag_start(m, AG1)
        elif k == 7:
            ag_mid(m, AG1)
        else:
            ag_end(m, AG1)
            for key, copy in copies.items():
                if key[0] == m and key[1] in (AG2, AG1):
                    copy.wait_send()

    x_copies, pair_copies = {}, {}

    def x_copy(layer, stage, di, piece, src, dst):
        k = (stage * 2 + di) * 3 + piece
        copy = pltpu.make_async_remote_copy(src_ref=src, dst_ref=dst, send_sem=x_send.at[layer, k], recv_sem=x_recv.at[layer, k],
                                            device_id=neighbour("x", DIRS[di][1]), device_id_type=MESH)
        x_copies[layer, stage, di, piece] = copy
        return copy

    def pair_copy(layer, k, src, dst):
        return pltpu.make_async_remote_copy(src_ref=src, dst_ref=dst, send_sem=pair_send.at[layer, k], recv_sem=pair_recv.at[layer, k],
                                            device_id=partner, device_id_type=MESH)

    def chunk(j, half=None):
        base = core * HALF + j * TOK
        if half is None:
            return pl.ds(pl.multiple_of(base, TOK), TOK)
        return pl.ds(pl.multiple_of(base + half * (TOK // 2), TOK // 2), TOK // 2)

    def block(g_buf, p_buf, row, keep_gelu):
        toks = pl.ds(pl.multiple_of(row, TOK), TOK)
        act_grad = lax.dot_general(g_buf[toks, :], wd_buf[...], (((1,), (1,)), ((), ())), preferred_element_type=F32)
        gelu_out, gelu_slope = gelu_parts(h_buf[toks, :].astype(F32))
        hid_grad = (act_grad * gelu_slope).astype(BF16)
        dh_buf[toks, :] = hid_grad
        if keep_gelu:
            h_buf[toks, :] = gelu_out.astype(BF16)
        p_buf[toks, :] = lax.dot_general(hid_grad, wu_buf[...], (((1,), (1,)), ((), ())), preferred_element_type=F32).astype(BF16)

    def hidden_grads(layer, g_buf, p_buf, keep_gelu):
        for di, step in DIRS:
            far, near = wrap(pos["x"] + 2), wrap(pos["x"] + step)
            x_copy(layer, 0, di, 0, p_buf.at[chunk(far, di)], xring.at[di, 0])
            x_copy(layer, 0, di, 1, p_buf.at[chunk(near, 1 - di)], xring.at[di, 1])

        @pl.loop(0, 4)
        def _(i):
            j = lax.rem(pos["x"] + 2 + i, 4)
            other = pl.multiple_of((1 - core) * HALF + j * TOK, TOK)
            block(g_buf, p_buf, other, keep_gelu)
            landing = pair_in.at[pl.ds(pl.multiple_of(j * TOK, TOK), TOK)]
            copy = pair_copy(layer, i, p_buf.at[pl.ds(other, TOK)], landing)
            copy.start()
            block(g_buf, p_buf, pl.multiple_of(core * HALF + j * TOK, TOK), keep_gelu)
            copy.wait()
            p_buf[chunk(j), :] = (p_buf[chunk(j), :].astype(F32) + landing[...].astype(F32)).astype(BF16)

            @pl.when(i == 0)
            def _():
                for di, _ in DIRS:
                    x_copies[layer, 0, di, 0].start()

            @pl.when(i == 1)
            def _():
                x_copies[layer, 0, 1, 1].start()

            @pl.when(i == 3)
            def _():
                x_copies[layer, 0, 0, 1].start()

        pl.semaphore_signal(pair_free.at[layer], inc=1, device_id=partner, device_id_type=MESH)

    def tp_step(layer, k, g_buf, p_buf):
        if k == 0:
            for di, step in DIRS:
                x_copies[layer, 0, di, 0].wait_recv()
                near = chunk(wrap(pos["x"] + step), di)
                p_buf[near, :] = (p_buf[near, :].astype(F32) + xring[di, 0].astype(F32)).astype(BF16)
                x_copy(layer, 0, di, 2, p_buf.at[near], xring.at[di, 2]).start()
        elif k == 1:
            for di, _ in DIRS:
                x_copies[layer, 0, di, 1].wait_recv()
                x_copies[layer, 0, di, 2].wait_recv()
            for di, step in DIRS:
                for piece in range(3):
                    x_copies[layer, 0, di, piece].wait_send()
            for di, step in DIRS:
                pl.semaphore_signal(x_free.at[layer, di], inc=1, device_id=neighbour("x", -step), device_id_type=MESH)
            for di, _ in DIRS:
                own = chunk(pos["x"], di)
                total = p_buf[own, :].astype(F32) + xring[di, 2].astype(F32) + xring[1 - di, 1].astype(F32)
                p_buf[own, :] = (g_buf[own, :].astype(F32) + total).astype(BF16)
            for piece in range(2):
                for di, _ in DIRS:
                    if piece == 0:
                        pl.semaphore_wait(x_free.at[layer, di], 1)
                    part = p_buf.at[chunk(pos["x"], di if piece == 0 else 1 - di)]
                    x_copy(layer, 1, di, piece, part, part).start()
            pl.semaphore_wait(pair_free.at[layer], 1)
            tp_forward(layer, 0, p_buf, pos["x"])
        elif k == 2:
            for di, step in DIRS:
                x_copies[layer, 1, di, 0].wait_recv()
                part = p_buf.at[chunk(wrap(pos["x"] - step), di)]
                x_copy(layer, 1, di, 2, part, part).start()
        elif k == 3:
            for di, step in DIRS:
                x_copies[layer, 1, di, 1].wait_recv()
                tp_forward(layer, 1 + di, p_buf, wrap(pos["x"] - step))
        elif k == 4:
            for di, _ in DIRS:
                x_copies[layer, 1, di, 2].wait_recv()
            tp_forward(layer, 3, p_buf, wrap(pos["x"] + 2))
        else:
            for k in range(4):
                pair_copies[layer, k].wait()
            for key, copy in x_copies.items():
                if key[:2] == (layer, 1):
                    copy.wait_send()

    def tp_forward(layer, k, p_buf, j):
        part = p_buf.at[chunk(j)]
        copy = pair_copy(layer, 4 + k, part, part)
        copy.start()
        pair_copies[layer, k] = copy

    def down_grad(m, gelu_buf, g_buf):
        w = weight_sums[m]

        @pl.loop(0, F // 256)
        def _(i):
            at = pl.ds(pl.multiple_of(i * 256, 256), 256)
            for half in range(2):
                w[half, at, :] = lax.dot_general(gelu_buf[:, at], g_buf[:, half * F:(half + 1) * F], (((0,), (0,)), ((), ())), preferred_element_type=F32)

    def x_load(layer, i):
        return pltpu.make_async_copy(x_hbm.at[layer, 0, :, pl.ds(pl.multiple_of(i * 256, 256), 256)], x_tile.at[lax.rem(i, 2)], x_sem.at[lax.rem(i, 2)])

    def up_grad_begin(layer):
        x_load(layer, 0).start()
        x_load(layer, 1).start()

    def up_grad(m, layer):
        w = weight_sums[m]

        @pl.loop(0, D // 256)
        def _(i):
            x_load(layer, i).wait()
            w[i // 3, pl.ds(pl.multiple_of(lax.rem(i, 3) * 256, 256), 256), :] = lax.dot_general(
                x_tile[lax.rem(i, 2)], dh_buf[...], (((0,), (0,)), ((), ())), preferred_element_type=F32)

            @pl.when(i + 2 < D // 256)
            def _():
                x_load(layer, i + 2).start()

    up_grad_begin(1)
    load_h.wait()

    @pl.loop(0, T // 256)
    def _(i):
        toks = pl.ds(pl.multiple_of(i * 256, 256), 256)
        dh_buf[toks, :] = gelu_parts(h_buf[toks, :].astype(F32))[0].astype(BF16)

    load_g.wait()
    down_grad(0, dh_buf, buf_a)
    pl.semaphore_wait(barrier, 7)
    dp_step(0, 0)
    load_wd.wait()
    load_wu.wait()
    hidden_grads(1, buf_a, buf_b, False)
    dp_step(0, 1)
    tp_step(1, 0, buf_a, buf_b)
    load_h = load(h_hbm.at[0, 0], h_buf, 0)
    load_wd = load(wd_hbm.at[0], wd_buf, 2)
    load_wu = load(wu_hbm.at[0], wu_buf, 3)
    up_grad(1, 1)
    up_grad_begin(0)
    dp_step(0, 2)
    dp_step(1, 0)
    dp_step(0, 3)
    tp_step(1, 1, buf_a, buf_b)
    dp_step(1, 1)
    dp_step(0, 4)
    tp_step(1, 2, buf_a, buf_b)
    dp_step(1, 2)
    dp_step(0, 5)
    tp_step(1, 3, buf_a, buf_b)
    dp_step(1, 3)
    dp_step(0, 6)
    dp_step(1, 4)
    tp_step(1, 4, buf_a, buf_b)
    dp_step(1, 5)
    tp_step(1, 5, buf_a, buf_b)
    load_h.wait()
    load_wd.wait()
    load_wu.wait()
    dp_step(0, 7)
    dp_step(1, 6)
    hidden_grads(0, buf_b, buf_a, True)
    dp_step(1, 7)
    tp_step(0, 0, buf_b, buf_a)
    down_grad(2, h_buf, buf_b)
    dp_step(0, 8)
    dp_step(2, 0)
    up_grad(3, 0)
    dp_step(1, 8)
    dp_step(2, 1)
    dp_step(3, 0)
    tp_step(0, 1, buf_b, buf_a)
    dp_step(2, 2)
    dp_step(3, 1)
    dp_step(2, 3)
    tp_step(0, 2, buf_b, buf_a)
    dp_step(3, 2)
    dp_step(2, 4)
    dp_step(3, 3)
    tp_step(0, 3, buf_b, buf_a)
    dp_step(2, 5)
    dp_step(3, 4)
    dp_step(2, 6)
    tp_step(0, 4, buf_b, buf_a)
    dp_step(3, 5)
    dp_step(2, 7)
    dp_step(3, 6)
    tp_step(0, 5, buf_b, buf_a)
    dp_step(3, 7)
    dp_step(2, 8)
    dp_step(3, 8)


def flush_kernel(g, w0, w1, w2, w3, g_out, up_out, down_out, sems):
    copies = [pltpu.make_async_copy(g, g_out.at[0], sems.at[0])]
    for layer, (down, up) in ((1, (w0, w1)), (0, (w2, w3))):
        for half in range(2):
            copies.append(pltpu.make_async_copy(up.at[half], up_out.at[layer, pl.ds(half * F, F)], sems.at[len(copies)]))
            copies.append(pltpu.make_async_copy(down.at[half], down_out.at[layer, :, pl.ds(half * F, F)], sems.at[len(copies)]))
    for copy in copies:
        copy.start()
    for copy in copies:
        copy.wait()


def solution(mesh):
    hbm, vmem = pl.BlockSpec(memory_space=pl.ANY), pl.BlockSpec(memory_space=pltpu.VMEM)

    def run_backward(w_up, w_down, x_saved, h_saved, grad_out):
        parts = pl.pallas_call(
            backward_kernel,
            name="backward",
            out_shape=[pltpu.VMEM((T, D), BF16)] + [pltpu.VMEM((2, F, F), F32)] * 4,
            in_specs=[hbm] * 5,
            out_specs=[vmem] * 5,
            scratch_shapes=[
                pltpu.VMEM((T, D), BF16),
                pltpu.VMEM((HALF, D), BF16),
                pltpu.VMEM((T, F), BF16),
                pltpu.VMEM((T, F), BF16),
                pltpu.VMEM((D, F), BF16),
                pltpu.VMEM((F, D), BF16),
                pltpu.VMEM((2, T, 256), BF16),
                pltpu.VMEM((2, 2, 2, 3, N1, F), F32),
                pltpu.VMEM((2, 2, 2, 3, N2, F), F32),
                pltpu.VMEM((2, 3, TOK // 2, D), BF16),
                pltpu.SemaphoreType.DMA((4, 48)),
                pltpu.SemaphoreType.DMA((4, 48)),
                pltpu.SemaphoreType.REGULAR((4, 2, 2, 2)),
                pltpu.SemaphoreType.DMA((2, 12)),
                pltpu.SemaphoreType.DMA((2, 12)),
                pltpu.SemaphoreType.REGULAR((2, 2)),
                pltpu.SemaphoreType.DMA((2, 8)),
                pltpu.SemaphoreType.DMA((2, 8)),
                pltpu.SemaphoreType.REGULAR((2,)),
                pltpu.SemaphoreType.DMA((4,)),
                pltpu.SemaphoreType.DMA((2,)),
            ],
            compiler_params=pltpu.CompilerParams(collective_id=0, has_side_effects=True, vmem_limit_bytes=41800000),
        )(w_up, w_down, x_saved, h_saved, grad_out)
        grad_in, up_total, down_total = pl.pallas_call(
            flush_kernel,
            name="flush",
            out_shape=[jax.ShapeDtypeStruct((1, T, D), BF16), jax.ShapeDtypeStruct((2, D, F), F32), jax.ShapeDtypeStruct((2, F, D), F32)],
            in_specs=[vmem] * 5,
            out_specs=[hbm] * 3,
            scratch_shapes=[pltpu.SemaphoreType.DMA((9,))],
            compiler_params=pltpu.CompilerParams(vmem_limit_bytes=1 << 20),
        )(*parts)
        return grad_in, up_total, down_total

    return jax.shard_map(run_backward, mesh=mesh, in_specs=(P(None, None, "tp"), P(None, "tp", None), P(None, "dp", None, None), P(None, "dp", None, "tp"), P("dp", None, None)), out_specs=(P("dp", None, None), P(None, None, "tp"), P(None, "tp", None)), check_vma=False)
```

time: 489 us -> 233 us (0.48)
  waiting for transfers between devices: 353 us -> 0 us
  Pallas kernels: 0 us -> 232 us
  matrix products: 79.7 us -> 0 us
  other arithmetic: 23.3 us -> 0 us
  local copies, waits for them, and re-layouts: 17.9 us -> 0 us
  between operations: 13.8 us -> 0.8 us
    psum x3 -> x0, waiting for transfers between devices: 353 us -> none  [the longest x1 234 us: run_backward(): lax.psum(jnp.stack([up_grads[layer_idx] for layer_idx in range(layer_coun...]
    pallas_call x0 -> x2, Pallas kernels: none -> 232 us  [the longest x1 223 us: run_backward(): pl.pallas_call(backward_kernel, name='backward', out_shape=[pltpu.VMEM((T...]
    dot_general x8 -> x0, matrix products: 79.7 us -> none  [the longest x2 25.1 us: run_backward(): jnp.einsum('bsd,fd->bsf', grad_cur, w_down[layer_idx], preferred_element_...]
    unnamed x8 -> x0, local copies, waits for them, and re-layouts: 17.9 us -> none
    another operation x2 -> x0, other arithmetic: 11.7 us -> none  [the longest x1 7.08 us: run_backward(): jnp.stack([up_grads[layer_idx] for layer_idx in range(layer_count)])]
    convert_element_type x1 -> x0, other arithmetic: 11.6 us -> none  [run_backward(): (grad_cur.astype(jnp.float32) + full_sum.astype(jnp.float32)).astype(jnp....]
  transfers between devices with their start and end apart: 3 -> 0, of which waited for: 3 -> 0; matrix products, arithmetic and copies ran while one was open for 13% -> 0% of each run, Pallas kernels for 0% -> 0%
where the time goes in v1:
time: 233 us
  Pallas kernels  232 us (100%)
    pallas_call x1, Pallas kernels, run_backward(): pl.pallas_call(backward_kernel, name='backward', out_shape=[pltpu.VMEM((T...  223 us
    pallas_call x1, Pallas kernels, run_backward(): pl.pallas_call(flush_kernel, name='flush', out_shape=[jax.ShapeDtypeStruc...  8.53 us

profile of v1, /device:TPU:0, one launch (start us, length us, event | category | flops | bytes accessed | tf_op | source)
XLA Modules:
  0.0 232.8 jit_solution(12596710035018925435)
XLA Ops:
  0.6 223.5 %backward.1 = (bf16[2048,1536]{1,0:T(8,128)(2,1)S(1)}, f32[2,768,768]{2,1,0:T(8,128)S(1)}, f32[2,768,768]{2,1,0:T(8,128)S(1)}, f32[2,768,768]{2,1,0:T(8,128)S(1)}, f32[2,768,768]{2,1,0:T(8,128)S(1)}) custom-call(bf16[2,1536,768]{2,1,0:T(8,128)(2,1)} %wu_hbm.1, bf16[2,768,1536]{2,1,0:T(8,128)(2,1)} %wd_hbm.1, bf16[2,1,2048,1536]{3,2,1,0:T(8,128)(2,1)} %x_hbm.1, ...), custom_call_target="tpu_custom_call" | custom-call | tf_op jit(solution)/shard_map/backward/pallas_call | solution.py:408
  224.1 8.5 %flush.1 = (bf16[1,2048,1536]{2,1,0:T(8,128)(2,1)}, f32[2,1536,768]{2,1,0:T(8,128)}, f32[2,768,1536]{2,1,0:T(8,128)}) custom-call(bf16[2048,1536]{1,0:T(8,128)(2,1)S(1)} %get-tuple-element.8.g, f32[2,768,768]{2,1,0:T(8,128)S(1)} %get-tuple-element.9.w0, f32[2,768,768]{2,1,0:T(8,128)S(1)} %get-tuple-element.10.w1, f32[2,768,768]{2,1,0:T(8,128)S(1)} %get-tuple-element.11.w2, ...), custom_call_target="tpu_custom_call" | custom-call | tf_op jit(solution)/shard_map/flush/pallas_call | solution.py:439

commit v2 on v0

v2 whole, which is shorter than its diff:
```python
import jax
import jax.numpy as jnp
from jax import lax
from jax.experimental import pallas as pl
from jax.experimental.pallas import tpu as pltpu
from jax.sharding import PartitionSpec as P

MESH = pl.DeviceIdType.MESH
F32, BF16 = jnp.float32, jnp.bfloat16
T, D, F = 2048, 1536, 768
HALF = T // 2
TOK = HALF // 4
Q = F // 2
N1, N2 = F // 8, F // 32
PARTS = 8
SLOTS = 4
RS1, RS2, AG2, AG1 = range(4)
DIRS = ((0, 1), (1, -1))

ORDER = (
    "DbaaDddcHHbbacHdcHabUfeeTdUfcgaebfhhdggcTehbfecdabghfecdahgT",
    "bfdechTfagbbaheccTddfTHHbaegfhheHHaDjgighUDjjhfdiillUpjTgicp",
    "kjemmkpjifnlkipnjmnTpgoikljpmnipkjlomknTolpnkmiojnlimkTopnjm",
    "kopmmolloklnTnookolTpnim",
)


def gelu_parts(hidden):
    tanh_val = jnp.tanh(0.7978845608028654 * (hidden + 0.044715 * hidden * hidden * hidden))
    gelu_out = 0.5 * hidden * (1.0 + tanh_val)
    gelu_slope = 0.5 * (1.0 + tanh_val) + 0.5 * hidden * (1.0 - tanh_val * tanh_val) * 0.7978845608028654 * (1.0 + 0.134145 * hidden * hidden)
    return gelu_out, gelu_slope


def backward_kernel(wu_hbm, wd_hbm, x_hbm, h_hbm, g_hbm, buf_a, *refs):
    sums = refs[:PARTS]
    (buf_b, pair_in, h_buf, dh_buf, wu_buf, wd_buf, x_tile, ring1, ring2, xring,
     dp_send, dp_recv, dp_free, x_send, x_recv, x_free, pair_send, pair_recv, pair_free, load_sem, x_sem) = refs[PARTS:]
    dp_pos, tp_pos = lax.axis_index("dp"), lax.axis_index("tp")
    core = lax.rem(tp_pos, 2)
    pos = {"x": tp_pos // 2, "y": lax.rem(dp_pos, 4), "z": dp_pos // 4}
    g_of, p_of = {1: buf_a, 0: buf_b}, {1: buf_b, 0: buf_a}

    def wrap(value):
        return lax.rem(value + 4, 4)

    def neighbour(axis, step):
        moved = wrap(pos[axis] + step)
        if axis == "x":
            return {"dp": dp_pos, "tp": moved * 2 + core}
        if axis == "y":
            return {"dp": pos["z"] * 4 + moved, "tp": tp_pos}
        return {"dp": moved * 4 + pos["y"], "tp": tp_pos}

    partner = {"dp": dp_pos, "tp": pos["x"] * 2 + 1 - core}

    def load(src, dst, k):
        copy = pltpu.make_async_copy(src, dst, load_sem.at[k])
        copy.start()
        return copy

    def x_load(layer, i):
        slot = lax.rem(i, 2)
        return pltpu.make_async_copy(x_hbm.at[layer, 0, :, pl.ds(pl.multiple_of(i * 256, 256), 256)], x_tile.at[slot], x_sem.at[slot])

    h_rows = [pl.ds(i * (T // 4), T // 4) for i in range(4)]
    load_h = [load(h_hbm.at[1, 0, h_rows[i]], h_buf.at[h_rows[i]], i) for i in range(4)]
    load_g = [load(g_hbm.at[0, :, pl.ds(i * F, F)], buf_a.at[:, pl.ds(i * F, F)], 4 + i) for i in range(2)]
    load_w = [load(wd_hbm.at[1], wd_buf, 6), load(wu_hbm.at[1], wu_buf, 7)]
    x_load(1, 0).start()
    x_load(1, 1).start()

    barrier = pltpu.get_barrier_semaphore()
    for axis in "xyz":
        for _, step in DIRS:
            pl.semaphore_signal(barrier, inc=1, device_id=neighbour(axis, step), device_id_type=MESH)
    pl.semaphore_signal(barrier, inc=1, device_id=partner, device_id_type=MESH)

    def remote(src, dst, send_sem, recv_sem, device):
        return pltpu.make_async_remote_copy(src_ref=src, dst_ref=dst, send_sem=send_sem, recv_sem=recv_sem, device_id=device, device_id_type=MESH)

    def dp_axes(stage, colour):
        first, second = ("y", "z") if colour == 0 else ("z", "y")
        return first if stage in (RS1, AG1) else second

    def dp_rows(stage, colour, j):
        if stage in (RS1, AG1):
            return pl.ds(pl.multiple_of(colour * (F // 2) + j * N1, 8), N1)
        return pl.ds(pl.multiple_of(colour * (F // 2) + pos[dp_axes(RS1, colour)] * N1 + j * N2, 8), N2)

    def dp_ring(n, stage, colour):
        return (ring1 if stage in (RS1, AG1) else ring2).at[n % SLOTS, colour]

    def dp_copy(n, stage, colour, di, piece):
        w, axis, step = sums[n], dp_axes(stage, colour), DIRS[di][1]
        p = pos[axis]
        if stage in (RS1, RS2):
            dst = dp_ring(n, stage, colour).at[di, piece]
            if piece == 0:
                src = w.at[di, dp_rows(stage, colour, wrap(p + 2))]
            else:
                src = w.at[1 - di if piece == 1 else di, dp_rows(stage, colour, wrap(p + step))]
        else:
            j = p if piece < 2 else wrap(p - step)
            src = dst = w.at[1 - di if piece == 1 else di, dp_rows(stage, colour, j)]
        return remote(src, dst, dp_send.at[n % SLOTS, stage, colour], dp_recv.at[n % SLOTS, stage, colour, min(piece, 1)], neighbour(axis, step))

    def dp_received(n, stage, colour, last):
        ring = dp_ring(n, stage, colour)
        pieces = ring.at[:, pl.ds(1, 2)] if last else ring.at[:, pl.ds(0, 1)]
        remote(pieces, pieces, dp_send.at[n % SLOTS, stage, colour], dp_recv.at[n % SLOTS, stage, colour, last], partner).wait_recv()

    def dp_sent(n, stage, colour):
        ring = dp_ring(n, stage, colour)
        remote(ring, ring, dp_send.at[n % SLOTS, stage, colour], dp_recv.at[n % SLOTS, stage, colour, 0], partner).wait_send()

    def both(n, stage, colour, piece):
        for di, _ in DIRS:
            dp_copy(n, stage, colour, di, piece).start()

    def rs_mid(n, stage, colour):
        w, axis, ring = sums[n], dp_axes(stage, colour), dp_ring(n, stage, colour)
        dp_received(n, stage, colour, 0)
        for di, step in DIRS:
            near = dp_rows(stage, colour, wrap(pos[axis] + step))
            w[di, near, :] = w[di, near, :] + ring[di, 0]
            dp_copy(n, stage, colour, di, 2).start()

    def rs_end(n, stage, colour):
        w, axis, ring = sums[n], dp_axes(stage, colour), dp_ring(n, stage, colour)
        dp_received(n, stage, colour, 1)
        own = dp_rows(stage, colour, pos[axis])
        for di, _ in DIRS:
            w[di, own, :] = w[di, own, :] + ring[di, 2] + ring[1 - di, 1]

    def rs_free(n, stage, colour):
        dp_sent(n, stage, colour)
        for _, step in DIRS:
            pl.semaphore_signal(dp_free.at[n, stage, colour], inc=1, device_id=neighbour(dp_axes(stage, colour), step), device_id_type=MESH)

    def ag_ready(n, stage, colour):
        pl.semaphore_wait(dp_free.at[n, RS2 if stage == AG2 else RS1, colour], 2)

    def ag_mid(n, stage, colour):
        dp_received(n, stage, colour, 0)
        both(n, stage, colour, 2)

    def dp_step(n, colour, k):
        if k < 2:
            both(n, RS1, colour, k)
        elif k == 2:
            rs_mid(n, RS1, colour)
        elif k == 3:
            rs_end(n, RS1, colour)
            both(n, RS2, colour, 0)
            both(n, RS2, colour, 1)
            rs_free(n, RS1, colour)
        elif k == 4:
            rs_mid(n, RS2, colour)
        elif k == 5:
            rs_end(n, RS2, colour)
            rs_free(n, RS2, colour)
            ag_ready(n, AG2, colour)
            both(n, AG2, colour, 0)
            both(n, AG2, colour, 1)
        elif k == 6:
            ag_mid(n, AG2, colour)
        elif k == 7:
            dp_received(n, AG2, colour, 1)
            ag_ready(n, AG1, colour)
            both(n, AG1, colour, 0)
        elif k == 8:
            both(n, AG1, colour, 1)
        elif k == 9:
            ag_mid(n, AG1, colour)
        else:
            dp_received(n, AG1, colour, 1)
            dp_sent(n, AG2, colour)
            dp_sent(n, AG1, colour)

    def chunk(j, half=None):
        base = core * HALF + j * TOK
        if half is None:
            return pl.ds(pl.multiple_of(base, TOK), TOK)
        return pl.ds(pl.multiple_of(base + half * (TOK // 2), TOK // 2), TOK // 2)

    def x_copy(layer, stage, di, piece):
        p_buf, step, p = p_of[layer], DIRS[di][1], pos["x"]
        if stage == 0:
            dst = xring.at[di, piece]
            src = p_buf.at[chunk(wrap(p + 2), di) if piece == 0 else chunk(wrap(p + step), 1 - di if piece == 1 else di)]
        else:
            src = dst = p_buf.at[chunk(p if piece < 2 else wrap(p - step), 1 - di if piece == 1 else di)]
        recv = min(piece, 1) if stage == 0 else 2 + piece
        return remote(src, dst, x_send.at[layer, stage], x_recv.at[layer, recv], neighbour("x", step))

    def x_received(layer, recv):
        pieces = xring.at[:, pl.ds(1, 2)] if recv == 1 else xring.at[:, pl.ds(0, 1)]
        remote(pieces, pieces, x_send.at[layer, 0], x_recv.at[layer, recv], partner).wait_recv()

    def x_sent(layer, stage):
        remote(xring, xring, x_send.at[layer, stage], x_recv.at[layer, 0], partner).wait_send()

    def pair_copy(layer, k, src, dst):
        return remote(src, dst, pair_send.at[layer, k], pair_recv.at[layer, k], partner)

    def tp_forward(layer, k):
        part = p_of[layer].at[chunk(wrap(pos["x"] + (0, -1, 1, 2)[k]))]
        return pair_copy(layer, 4, part, part)

    def block(layer, row):
        toks = pl.ds(pl.multiple_of(row, TOK), TOK)
        act_grad = lax.dot_general(g_of[layer][toks, :], wd_buf[...], (((1,), (1,)), ((), ())), preferred_element_type=F32)
        gelu_out, gelu_slope = gelu_parts(h_buf[toks, :].astype(F32))
        hid_grad = (act_grad * gelu_slope).astype(BF16)
        dh_buf[toks, :] = hid_grad
        if layer == 0:
            h_buf[toks, :] = gelu_out.astype(BF16)
        p_of[layer][toks, :] = lax.dot_general(hid_grad, wu_buf[...], (((1,), (1,)), ((), ())), preferred_element_type=F32).astype(BF16)

    def hidden_grads(layer, hooks):
        p_buf = p_of[layer]

        @pl.loop(0, 4)
        def _(i):
            j = lax.rem(pos["x"] + 2 + i, 4)
            other = pl.multiple_of((1 - core) * HALF + j * TOK, TOK)
            block(layer, other)
            landing = pair_in.at[pl.ds(pl.multiple_of(j * TOK, TOK), TOK)]
            copy = pair_copy(layer, i, p_buf.at[pl.ds(other, TOK)], landing)
            copy.start()
            block(layer, pl.multiple_of(core * HALF + j * TOK, TOK))
            copy.wait()
            p_buf[chunk(j), :] = (p_buf[chunk(j), :].astype(F32) + landing[...].astype(F32)).astype(BF16)
            for k in range(4):

                @pl.when(i == k)
                def _():
                    if k == 0:
                        x_copy(layer, 0, 0, 0).start()
                        x_copy(layer, 0, 1, 0).start()
                    elif k == 1:
                        x_copy(layer, 0, 1, 1).start()
                    elif k == 3:
                        x_copy(layer, 0, 0, 1).start()
                        pl.semaphore_signal(pair_free.at[layer], inc=1, device_id=partner, device_id_type=MESH)
                    for op in hooks[k]:
                        run(op)

    def tp_step(layer, k):
        g_buf, p_buf = g_of[layer], p_of[layer]
        if k == 0:
            x_received(layer, 0)
            for di, step in DIRS:
                near = chunk(wrap(pos["x"] + step), di)
                p_buf[near, :] = (p_buf[near, :].astype(F32) + xring[di, 0].astype(F32)).astype(BF16)
                x_copy(layer, 0, di, 2).start()
        elif k == 1:
            x_received(layer, 1)
            x_sent(layer, 0)
            for _, step in DIRS:
                pl.semaphore_signal(x_free.at[layer], inc=1, device_id=neighbour("x", step), device_id_type=MESH)
            for di, _ in DIRS:
                own = chunk(pos["x"], di)
                total = p_buf[own, :].astype(F32) + xring[di, 2].astype(F32) + xring[1 - di, 1].astype(F32)
                p_buf[own, :] = (g_buf[own, :].astype(F32) + total).astype(BF16)
            pl.semaphore_wait(x_free.at[layer], 2)
            for piece in range(2):
                for di, _ in DIRS:
                    x_copy(layer, 1, di, piece).start()
            pl.semaphore_wait(pair_free.at[layer], 1)
            tp_forward(layer, 0).start()
        elif k == 2:
            x_received(layer, 2)
            for di, _ in DIRS:
                x_copy(layer, 1, di, 2).start()
        elif k == 3:
            x_received(layer, 3)
            tp_forward(layer, 1).start()
            tp_forward(layer, 2).start()
        elif k == 4:
            x_received(layer, 4)
            tp_forward(layer, 3).start()
        else:
            pair_copy(layer, 4, pair_in, pair_in).wait()
            x_sent(layer, 1)

    def put(w, at, value):
        w[0, at, :] = value[:, :Q]
        w[1, at, :] = value[:, Q:]

    def down_grad(layer, half):
        gelu_buf, g_buf = (dh_buf, buf_a) if layer == 1 else (h_buf, buf_b)

        @pl.loop(0, F // 256)
        def _(i):
            at = pl.ds(pl.multiple_of(i * 256, 256), 256)
            put(sums[(1 - layer) * 4 + half], at,
                lax.dot_general(gelu_buf[:, at], g_buf[:, half * F:(half + 1) * F], (((0,), (0,)), ((), ())), preferred_element_type=F32))

    def up_grad(layer, half):
        @pl.loop(0, F // 256)
        def _(t):
            i = half * (F // 256) + t
            x_load(layer, i).wait()
            put(sums[(1 - layer) * 4 + 2 + half], pl.ds(pl.multiple_of(t * 256, 256), 256),
                lax.dot_general(x_tile[lax.rem(i, 2)], dh_buf[...], (((0,), (0,)), ((), ())), preferred_element_type=F32))

            @pl.when(i + 2 < D // 256)
            def _():
                x_load(layer, i + 2).start()

        if layer == 1 and half == 1:
            x_load(0, 0).start()
            x_load(0, 1).start()

    taken = {}

    def run(letter):
        count = taken[letter] = taken.get(letter, -1) + 1
        if letter == "D":
            down_grad(1 - count // 2, count % 2)
        elif letter == "U":
            up_grad(1 - count // 2, count % 2)
        elif letter == "T":
            tp_step(1 - count // 6, count % 6)
        else:
            part = ord(letter) - ord("a")
            dp_step(part // 2, part % 2, count)

    for i in range(4):
        load_h[i].wait()

        @pl.loop(2 * i, 2 * i + 2)
        def _(b):
            toks = pl.ds(pl.multiple_of(b * 256, 256), 256)
            dh_buf[toks, :] = gelu_parts(h_buf[toks, :].astype(F32))[0].astype(BF16)

    todo = list("".join(ORDER))
    layer = 1
    for half in range(2):
        load_g[half].wait()
        while todo[0] != "D":
            run(todo.pop(0))
        run(todo.pop(0))
        if half == 0:
            pl.semaphore_wait(barrier, 7)
    while todo:
        if todo[0] != "H":
            run(todo.pop(0))
            continue
        hooks = []
        while len(hooks) < 4:
            letter = todo.pop(0)
            if letter == "H":
                hooks.append([])
            else:
                hooks[-1].append(letter)
        for copy in load_w + ([] if layer == 1 else load_h):
            copy.wait()
        hidden_grads(layer, hooks)
        if layer == 1:
            layer = 0
            load_h = [load(h_hbm.at[0, 0], h_buf, 0)]
            load_w = [load(wd_hbm.at[0], wd_buf, 6), load(wu_hbm.at[0], wu_buf, 7)]


def flush_kernel(g, *refs):
    sums, (g_out, up_out, down_out, sems) = refs[:PARTS], refs[PARTS:]
    copies = []
    for n in range(PARTS):
        layer, half = 1 - n // 4, n % 2
        for q in range(2):
            if n % 4 < 2:
                dst = down_out.at[layer, :, pl.ds(half * F + q * Q, Q)]
            else:
                dst = up_out.at[layer, pl.ds(half * F, F), pl.ds(q * Q, Q)]
            copies.append(pltpu.make_async_copy(sums[n].at[q], dst, sems.at[len(copies)]))
    copies.append(pltpu.make_async_copy(g, g_out.at[0], sems.at[len(copies)]))
    for copy in copies:
        copy.start()
    for copy in copies:
        copy.wait()


def solution(mesh):
    hbm, vmem = pl.BlockSpec(memory_space=pl.ANY), pl.BlockSpec(memory_space=pltpu.VMEM)
    dma, regular = pltpu.SemaphoreType.DMA, pltpu.SemaphoreType.REGULAR

    def run_backward(w_up, w_down, x_saved, h_saved, grad_out):
        results = pl.pallas_call(
            backward_kernel,
            name="backward",
            out_shape=[pltpu.VMEM((T, D), BF16)] + [pltpu.VMEM((2, F, Q), F32)] * PARTS,
            in_specs=[hbm] * 5,
            out_specs=[vmem] * (1 + PARTS),
            scratch_shapes=[
                pltpu.VMEM((T, D), BF16),
                pltpu.VMEM((HALF, D), BF16),
                pltpu.VMEM((T, F), BF16),
                pltpu.VMEM((T, F), BF16),
                pltpu.VMEM((D, F), BF16),
                pltpu.VMEM((F, D), BF16),
                pltpu.VMEM((2, T, 256), BF16),
                pltpu.VMEM((SLOTS, 2, 2, 3, N1, Q), F32),
                pltpu.VMEM((SLOTS, 2, 2, 3, N2, Q), F32),
                pltpu.VMEM((2, 3, TOK // 2, D), BF16),
                dma((SLOTS, 4, 2)),
                dma((SLOTS, 4, 2, 2)),
                regular((PARTS, 2, 2)),
                dma((2, 2)),
                dma((2, 5)),
                regular((2,)),
                dma((2, 5)),
                dma((2, 5)),
                regular((2,)),
                dma((8,)),
                dma((2,)),
            ],
            compiler_params=pltpu.CompilerParams(collective_id=0, has_side_effects=True, vmem_limit_bytes=41800000),
        )(w_up, w_down, x_saved, h_saved, grad_out)
        grad_in, up_total, down_total = pl.pallas_call(
            flush_kernel,
            name="flush",
            out_shape=[jax.ShapeDtypeStruct((1, T, D), BF16), jax.ShapeDtypeStruct((2, D, F), F32), jax.ShapeDtypeStruct((2, F, D), F32)],
            in_specs=[vmem] * (1 + PARTS),
            out_specs=[hbm] * 3,
            scratch_shapes=[dma((2 * PARTS + 1,))],
            compiler_params=pltpu.CompilerParams(vmem_limit_bytes=1 << 20),
        )(*results)
        return grad_in, up_total, down_total

    return jax.shard_map(run_backward, mesh=mesh, in_specs=(P(None, None, "tp"), P(None, "tp", None), P(None, "dp", None, None), P(None, "dp", None, "tp"), P("dp", None, None)), out_specs=(P("dp", None, None), P(None, None, "tp"), P(None, "tp", None)), check_vma=False)
```

time: 489 us -> 221 us (0.45)
  waiting for transfers between devices: 353 us -> 0 us
  Pallas kernels: 0 us -> 220 us
  matrix products: 79.7 us -> 0 us
  other arithmetic: 23.3 us -> 0 us
  local copies, waits for them, and re-layouts: 17.9 us -> 0 us
  between operations: 13.8 us -> 0.8 us
    psum x3 -> x0, waiting for transfers between devices: 353 us -> none  [the longest x1 234 us: run_backward(): lax.psum(jnp.stack([up_grads[layer_idx] for layer_idx in range(layer_coun...]
    pallas_call x0 -> x2, Pallas kernels: none -> 220 us  [the longest x1 211 us: run_backward(): pl.pallas_call(backward_kernel, name='backward', out_shape=[pltpu.VMEM((T...]
    dot_general x8 -> x0, matrix products: 79.7 us -> none  [the longest x2 25.1 us: run_backward(): jnp.einsum('bsd,fd->bsf', grad_cur, w_down[layer_idx], preferred_element_...]
    unnamed x8 -> x0, local copies, waits for them, and re-layouts: 17.9 us -> none
    another operation x2 -> x0, other arithmetic: 11.7 us -> none  [the longest x1 7.08 us: run_backward(): jnp.stack([up_grads[layer_idx] for layer_idx in range(layer_count)])]
    convert_element_type x1 -> x0, other arithmetic: 11.6 us -> none  [run_backward(): (grad_cur.astype(jnp.float32) + full_sum.astype(jnp.float32)).astype(jnp....]
  transfers between devices with their start and end apart: 3 -> 0, of which waited for: 3 -> 0; matrix products, arithmetic and copies ran while one was open for 13% -> 0% of each run, Pallas kernels for 0% -> 0%
where the time goes in v2:
time: 221 us
  Pallas kernels  220 us (100%)
    pallas_call x1, Pallas kernels, run_backward(): pl.pallas_call(backward_kernel, name='backward', out_shape=[pltpu.VMEM((T...  211 us
    pallas_call x1, Pallas kernels, run_backward(): pl.pallas_call(flush_kernel, name='flush', out_shape=[jax.ShapeDtypeStruc...  8.67 us

profile of v2, /device:TPU:0, one launch (start us, length us, event | category | flops | bytes accessed | tf_op | source)
XLA Modules:
  0.0 220.6 jit_solution(1829547554285653841)
XLA Ops:
  0.6 211.2 %backward.1 = (bf16[2048,1536]{1,0:T(8,128)(2,1)S(1)}, f32[2,768,384]{2,1,0:T(8,128)S(1)}, f32[2,768,384]{2,1,0:T(8,128)S(1)}, f32[2,768,384]{2,1,0:T(8,128)S(1)...) custom-call(bf16[2,1536,768]{2,1,0:T(8,128)(2,1)} %wu_hbm.1, ...), custom_call_target="tpu_custom_call" | custom-call | tf_op jit(solution)/shard_map/backward/pallas_call | solution.py:391
  211.8 8.7 %flush.1 = (bf16[1,2048,1536]{2,1,0:T(8,128)(2,1)}, f32[2,1536,768]{2,1,0:T(8,128)}, f32[2,768,1536]{2,1,0:T(8,128)}) custom-call(bf16[2048,1536]{1,0:T(8,128)(2,1)S(1)} %get-tuple-element.12.g, f32[2,768,384]{2,1,0:T(8,128)S(1)} %get-tuple-element.13.refs_0_, f32[2,768,384]{2,1,0:T(8,128)S(1)} %get-tuple-element.14.refs_1_, ...), custom_call_target="tpu_custom_call" | custom-call | tf_op jit(solution)/shard_map/flush/pallas_call | solution.py:422

commit v3 on v2

--- a/solution.py
+++ b/solution.py
@@ -18,18 +18,20 @@
 DIRS = ((0, 1), (1, -1))
 
 ORDER = (
-    "DbaaDddcHHbbacHdcHabUfeeTdUfcgaebfhhdggcTehbfecdabghfecdahgT",
-    "bfdechTfagbbaheccTddfTHHbaegfhheHHaDjgighUDjjhfdiillUpjTgicp",
-    "kjemmkpjifnlkipnjmnTpgoikljpmnipkjlomknTolpnkmiojnlimkTopnjm",
-    "kopmmolloklnTnookolTpnim",
+    "DaDbDcDHdabaHHcbHHdcHadHbHUeacUTfbUdagfbUhdaehegcbhdfTegchab",
+    "fehdgcTabfgehddcTfghceacdfTbgTHeheHHhHffbggHheHHaHcgfdDDDkjk",
+    "UDllfUngiiTkjilnemmTjlknUmijklUhpoomkjplomkijplTnTmkiojllpnk",
+    "opkmlnTpjmonlimjjopmkniTppioinpojomnpion",
 )
 
 
 def gelu_parts(hidden):
-    tanh_val = jnp.tanh(0.7978845608028654 * (hidden + 0.044715 * hidden * hidden * hidden))
-    gelu_out = 0.5 * hidden * (1.0 + tanh_val)
-    gelu_slope = 0.5 * (1.0 + tanh_val) + 0.5 * hidden * (1.0 - tanh_val * tanh_val) * 0.7978845608028654 * (1.0 + 0.134145 * hidden * hidden)
-    return gelu_out, gelu_slope
+    scale = 0.7978845608028654
+    square = hidden * hidden
+    tanh_val = jnp.tanh(hidden * (scale + (scale * 0.044715) * square))
+    upper = 0.5 + 0.5 * tanh_val
+    gelu_slope = upper + upper * (1.0 - tanh_val) * hidden * (scale + (scale * 0.134145) * square)
+    return hidden * upper, gelu_slope
 
 
 def backward_kernel(wu_hbm, wd_hbm, x_hbm, h_hbm, g_hbm, buf_a, *refs):
@@ -60,21 +62,24 @@
         return copy
 
     def x_load(layer, i):
-        slot = lax.rem(i, 2)
-        return pltpu.make_async_copy(x_hbm.at[layer, 0, :, pl.ds(pl.multiple_of(i * 256, 256), 256)], x_tile.at[slot], x_sem.at[slot])
-
-    h_rows = [pl.ds(i * (T // 4), T // 4) for i in range(4)]
-    load_h = [load(h_hbm.at[1, 0, h_rows[i]], h_buf.at[h_rows[i]], i) for i in range(4)]
-    load_g = [load(g_hbm.at[0, :, pl.ds(i * F, F)], buf_a.at[:, pl.ds(i * F, F)], 4 + i) for i in range(2)]
-    load_w = [load(wd_hbm.at[1], wd_buf, 6), load(wu_hbm.at[1], wu_buf, 7)]
-    x_load(1, 0).start()
-    x_load(1, 1).start()
+        slot = i % 2
+        return pltpu.make_async_copy(x_hbm.at[layer, 0, :, pl.ds(i * Q, Q)], x_tile.at[slot], x_sem.at[slot])
 
     barrier = pltpu.get_barrier_semaphore()
     for axis in "xyz":
         for _, step in DIRS:
             pl.semaphore_signal(barrier, inc=1, device_id=neighbour(axis, step), device_id_type=MESH)
     pl.semaphore_signal(barrier, inc=1, device_id=partner, device_id_type=MESH)
+
+    load_h, load_g = [], []
+    for i in range(2):
+        cols = pl.ds(i * Q, Q)
+        load_h.append(load(h_hbm.at[1, 0, :, cols], h_buf.at[:, cols], i))
+        cols = pl.ds(i * F, F)
+        load_g.append(load(g_hbm.at[0, :, cols], buf_a.at[:, cols], 2 + i))
+    load_w = [load(wd_hbm.at[1], wd_buf, 4), load(wu_hbm.at[1], wu_buf, 5)]
+    x_load(1, 0).start()
+    x_load(1, 1).start()
 
     def remote(src, dst, send_sem, recv_sem, device):
         return pltpu.make_async_remote_copy(src_ref=src, dst_ref=dst, send_sem=send_sem, recv_sem=recv_sem, device_id=device, device_id_type=MESH)
@@ -136,10 +141,10 @@
     def rs_free(n, stage, colour):
         dp_sent(n, stage, colour)
         for _, step in DIRS:
-            pl.semaphore_signal(dp_free.at[n, stage, colour], inc=1, device_id=neighbour(dp_axes(stage, colour), step), device_id_type=MESH)
+            pl.semaphore_signal(dp_free.at[n % SLOTS, stage, colour], inc=1, device_id=neighbour(dp_axes(stage, colour), step), device_id_type=MESH)
 
     def ag_ready(n, stage, colour):
-        pl.semaphore_wait(dp_free.at[n, RS2 if stage == AG2 else RS1, colour], 2)
+        pl.semaphore_wait(dp_free.at[n % SLOTS, RS2 if stage == AG2 else RS1, colour], 2)
 
     def ag_mid(n, stage, colour):
         dp_received(n, stage, colour, 0)
@@ -192,17 +197,17 @@
         else:
             src = dst = p_buf.at[chunk(p if piece < 2 else wrap(p - step), 1 - di if piece == 1 else di)]
         recv = min(piece, 1) if stage == 0 else 2 + piece
-        return remote(src, dst, x_send.at[layer, stage], x_recv.at[layer, recv], neighbour("x", step))
+        return remote(src, dst, x_send.at[stage], x_recv.at[recv], neighbour("x", step))
 
     def x_received(layer, recv):
         pieces = xring.at[:, pl.ds(1, 2)] if recv == 1 else xring.at[:, pl.ds(0, 1)]
-        remote(pieces, pieces, x_send.at[layer, 0], x_recv.at[layer, recv], partner).wait_recv()
+        remote(pieces, pieces, x_send.at[0], x_recv.at[recv], partner).wait_recv()
 
     def x_sent(layer, stage):
-        remote(xring, xring, x_send.at[layer, stage], x_recv.at[layer, 0], partner).wait_send()
+        remote(xring, xring, x_send.at[stage], x_recv.at[0], partner).wait_send()
 
     def pair_copy(layer, k, src, dst):
-        return remote(src, dst, pair_send.at[layer, k], pair_recv.at[layer, k], partner)
+        return remote(src, dst, pair_send.at[k], pair_recv.at[k], partner)
 
     def tp_forward(layer, k):
         part = p_of[layer].at[chunk(wrap(pos["x"] + (0, -1, 1, 2)[k]))]
@@ -229,10 +234,11 @@
             landing = pair_in.at[pl.ds(pl.multiple_of(j * TOK, TOK), TOK)]
             copy = pair_copy(layer, i, p_buf.at[pl.ds(other, TOK)], landing)
             copy.start()
+            run_hooks(i, hooks[0::2])
             block(layer, pl.multiple_of(core * HALF + j * TOK, TOK))
             copy.wait()
             p_buf[chunk(j), :] = (p_buf[chunk(j), :].astype(F32) + landing[...].astype(F32)).astype(BF16)
-            for k in range(4):
+            for k in (0, 1, 3):
 
                 @pl.when(i == k)
                 def _():
@@ -241,11 +247,20 @@
                         x_copy(layer, 0, 1, 0).start()
                     elif k == 1:
                         x_copy(layer, 0, 1, 1).start()
-                    elif k == 3:
+                    else:
                         x_copy(layer, 0, 0, 1).start()
-                        pl.semaphore_signal(pair_free.at[layer], inc=1, device_id=partner, device_id_type=MESH)
-                    for op in hooks[k]:
-                        run(op)
+                        pl.semaphore_signal(pair_free, inc=1, device_id=partner, device_id_type=MESH)
+
+            run_hooks(i, hooks[1::2])
+
+    def run_hooks(i, hooks):
+        for k in range(4):
+            if hooks[k]:
+
+                @pl.when(i == k)
+                def _():
+                    for letter in hooks[k]:
+                        run(letter)
 
     def tp_step(layer, k):
         g_buf, p_buf = g_of[layer], p_of[layer]
@@ -259,16 +274,16 @@
             x_received(layer, 1)
             x_sent(layer, 0)
             for _, step in DIRS:
-                pl.semaphore_signal(x_free.at[layer], inc=1, device_id=neighbour("x", step), device_id_type=MESH)
+                pl.semaphore_signal(x_free, inc=1, device_id=neighbour("x", step), device_id_type=MESH)
             for di, _ in DIRS:
                 own = chunk(pos["x"], di)
                 total = p_buf[own, :].astype(F32) + xring[di, 2].astype(F32) + xring[1 - di, 1].astype(F32)
                 p_buf[own, :] = (g_buf[own, :].astype(F32) + total).astype(BF16)
-            pl.semaphore_wait(x_free.at[layer], 2)
+            pl.semaphore_wait(x_free, 2)
             for piece in range(2):
                 for di, _ in DIRS:
                     x_copy(layer, 1, di, piece).start()
-            pl.semaphore_wait(pair_free.at[layer], 1)
+            pl.semaphore_wait(pair_free, 1)
             tp_forward(layer, 0).start()
         elif k == 2:
             x_received(layer, 2)
@@ -289,68 +304,56 @@
         w[0, at, :] = value[:, :Q]
         w[1, at, :] = value[:, Q:]
 
-    def down_grad(layer, half):
+    def down_grad(layer, half, colour):
         gelu_buf, g_buf = (dh_buf, buf_a) if layer == 1 else (h_buf, buf_b)
-
-        @pl.loop(0, F // 256)
-        def _(i):
-            at = pl.ds(pl.multiple_of(i * 256, 256), 256)
-            put(sums[(1 - layer) * 4 + half], at,
-                lax.dot_general(gelu_buf[:, at], g_buf[:, half * F:(half + 1) * F], (((0,), (0,)), ((), ())), preferred_element_type=F32))
-
-    def up_grad(layer, half):
-        @pl.loop(0, F // 256)
-        def _(t):
-            i = half * (F // 256) + t
-            x_load(layer, i).wait()
-            put(sums[(1 - layer) * 4 + 2 + half], pl.ds(pl.multiple_of(t * 256, 256), 256),
-                lax.dot_general(x_tile[lax.rem(i, 2)], dh_buf[...], (((0,), (0,)), ((), ())), preferred_element_type=F32))
-
-            @pl.when(i + 2 < D // 256)
-            def _():
-                x_load(layer, i + 2).start()
-
-        if layer == 1 and half == 1:
-            x_load(0, 0).start()
-            x_load(0, 1).start()
+        cols = pl.ds(colour * Q, Q)
+        if layer == 1 and half == 0:
+            load_h[colour].wait()
+
+            @pl.loop(0, T // 256)
+            def _(i):
+                toks = pl.ds(pl.multiple_of(i * 256, 256), 256)
+                dh_buf[toks, cols] = gelu_parts(h_buf[toks, cols].astype(F32))[0].astype(BF16)
+
+        if layer == 1 and colour == 0:
+            load_g[half].wait()
+        put(sums[(1 - layer) * 4 + half], cols,
+            lax.dot_general(gelu_buf[:, cols], g_buf[:, half * F:(half + 1) * F], (((0,), (0,)), ((), ())), preferred_element_type=F32))
+
+    def up_grad(layer, half, colour):
+        i = half * 2 + colour
+        x_load(layer, i).wait()
+        put(sums[(1 - layer) * 4 + 2 + half], pl.ds(colour * Q, Q),
+            lax.dot_general(x_tile[i % 2], dh_buf[...], (((0,), (0,)), ((), ())), preferred_element_type=F32))
+        if i < 2:
+            x_load(layer, i + 2).start()
+        elif layer == 1:
+            x_load(0, i - 2).start()
 
     taken = {}
 
     def run(letter):
         count = taken[letter] = taken.get(letter, -1) + 1
         if letter == "D":
-            down_grad(1 - count // 2, count % 2)
+            down_grad(1 - count // 4, count // 2 % 2, count % 2)
         elif letter == "U":
-            up_grad(1 - count // 2, count % 2)
+            up_grad(1 - count // 4, count // 2 % 2, count % 2)
         elif letter == "T":
             tp_step(1 - count // 6, count % 6)
         else:
             part = ord(letter) - ord("a")
             dp_step(part // 2, part % 2, count)
 
-    for i in range(4):
-        load_h[i].wait()
-
-        @pl.loop(2 * i, 2 * i + 2)
-        def _(b):
-            toks = pl.ds(pl.multiple_of(b * 256, 256), 256)
-            dh_buf[toks, :] = gelu_parts(h_buf[toks, :].astype(F32))[0].astype(BF16)
-
     todo = list("".join(ORDER))
     layer = 1
-    for half in range(2):
-        load_g[half].wait()
-        while todo[0] != "D":
-            run(todo.pop(0))
-        run(todo.pop(0))
-        if half == 0:
-            pl.semaphore_wait(barrier, 7)
+    run(todo.pop(0))
+    pl.semaphore_wait(barrier, 7)
     while todo:
         if todo[0] != "H":
             run(todo.pop(0))
             continue
         hooks = []
-        while len(hooks) < 4:
+        while len(hooks) < 8:
             letter = todo.pop(0)
             if letter == "H":
                 hooks.append([])
@@ -362,7 +365,7 @@
         if layer == 1:
             layer = 0
             load_h = [load(h_hbm.at[0, 0], h_buf, 0)]
-            load_w = [load(wd_hbm.at[0], wd_buf, 6), load(wu_hbm.at[0], wu_buf, 7)]
+            load_w = [load(wd_hbm.at[0], wd_buf, 4), load(wu_hbm.at[0], wu_buf, 5)]
 
 
 def flush_kernel(g, *refs):
@@ -401,20 +404,20 @@
                 pltpu.VMEM((T, F), BF16),
                 pltpu.VMEM((D, F), BF16),
                 pltpu.VMEM((F, D), BF16),
-                pltpu.VMEM((2, T, 256), BF16),
+                pltpu.VMEM((2, T, Q), BF16),
                 pltpu.VMEM((SLOTS, 2, 2, 3, N1, Q), F32),
                 pltpu.VMEM((SLOTS, 2, 2, 3, N2, Q), F32),
                 pltpu.VMEM((2, 3, TOK // 2, D), BF16),
                 dma((SLOTS, 4, 2)),
                 dma((SLOTS, 4, 2, 2)),
-                regular((PARTS, 2, 2)),
-                dma((2, 2)),
-                dma((2, 5)),
-                regular((2,)),
-                dma((2, 5)),
-                dma((2, 5)),
-                regular((2,)),
-                dma((8,)),
+                regular((SLOTS, 2, 2)),
+                dma((2,)),
+                dma((5,)),
+                regular,
+                dma((5,)),
+                dma((5,)),
+                regular,
+                dma((6,)),
                 dma((2,)),
             ],
             compiler_params=pltpu.CompilerParams(collective_id=0, has_side_effects=True, vmem_limit_bytes=41800000),

time: 221 us -> 216 us (0.977)
  Pallas kernels: 220 us -> 215 us
    pallas_call x1, Pallas kernels: 211 us -> 206 us  [run_backward(): pl.pallas_call(backward_kernel, name='backward', out_shape=[pltpu.VMEM((T...]
where the time goes in v3:
time: 216 us
  Pallas kernels  215 us (100%)
    pallas_call x1, Pallas kernels, run_backward(): pl.pallas_call(backward_kernel, name='backward', out_shape=[pltpu.VMEM((T...  206 us
    pallas_call x1, Pallas kernels, run_backward(): pl.pallas_call(flush_kernel, name='flush', out_shape=[jax.ShapeDtypeStruc...  8.67 us

profile of v3, /device:TPU:0, one launch (start us, length us, event | category | flops | bytes accessed | tf_op | source)
XLA Modules:
  0.0 215.6 jit_solution(13424455989145178112)
XLA Ops:
  0.6 206.1 %backward.1 = (bf16[2048,1536]{1,0:T(8,128)(2,1)S(1)}, f32[2,768,384]{2,1,0:T(8,128)S(1)}, f32[2,768,384]{2,1,0:T(8,128)S(1)}, f32[2,768,384]{2,1,0:T(8,128)S(1)...) custom-call(bf16[2,1536,768]{2,1,0:T(8,128)(2,1)} %wu_hbm.1, ...), custom_call_target="tpu_custom_call" | custom-call | tf_op jit(solution)/shard_map/backward/pallas_call | solution.py:394
  206.8 8.7 %flush.1 = (bf16[1,2048,1536]{2,1,0:T(8,128)(2,1)}, f32[2,1536,768]{2,1,0:T(8,128)}, f32[2,768,1536]{2,1,0:T(8,128)}) custom-call(bf16[2048,1536]{1,0:T(8,128)(2,1)S(1)} %get-tuple-element.12.g, f32[2,768,384]{2,1,0:T(8,128)S(1)} %get-tuple-element.13.refs_0_, f32[2,768,384]{2,1,0:T(8,128)S(1)} %get-tuple-element.14.refs_1_, ...), custom_call_target="tpu_custom_call" | custom-call | tf_op jit(solution)/shard_map/flush/pallas_call | solution.py:425

commit v4 on v3

--- a/solution.py
+++ b/solution.py
@@ -27,10 +27,10 @@
 
 def gelu_parts(hidden):
     scale = 0.7978845608028654
-    square = hidden * hidden
-    tanh_val = jnp.tanh(hidden * (scale + (scale * 0.044715) * square))
+    eighth = hidden * (0.125 * hidden)
+    tanh_val = jnp.tanh(hidden * (scale + (scale * 0.35772) * eighth))
     upper = 0.5 + 0.5 * tanh_val
-    gelu_slope = upper + upper * (1.0 - tanh_val) * hidden * (scale + (scale * 0.134145) * square)
+    gelu_slope = upper + upper * (1.0 - tanh_val) * hidden * (scale + (scale * 1.07316) * eighth)
     return hidden * upper, gelu_slope
 
 
@@ -64,12 +64,6 @@
     def x_load(layer, i):
         slot = i % 2
         return pltpu.make_async_copy(x_hbm.at[layer, 0, :, pl.ds(i * Q, Q)], x_tile.at[slot], x_sem.at[slot])
-
-    barrier = pltpu.get_barrier_semaphore()
-    for axis in "xyz":
-        for _, step in DIRS:
-            pl.semaphore_signal(barrier, inc=1, device_id=neighbour(axis, step), device_id_type=MESH)
-    pl.semaphore_signal(barrier, inc=1, device_id=partner, device_id_type=MESH)
 
     load_h, load_g = [], []
     for i in range(2):
@@ -80,6 +74,12 @@
     load_w = [load(wd_hbm.at[1], wd_buf, 4), load(wu_hbm.at[1], wu_buf, 5)]
     x_load(1, 0).start()
     x_load(1, 1).start()
+
+    barrier = pltpu.get_barrier_semaphore()
+    for axis in "xyz":
+        for _, step in DIRS:
+            pl.semaphore_signal(barrier, inc=1, device_id=neighbour(axis, step), device_id_type=MESH)
+    pl.semaphore_signal(barrier, inc=1, device_id=partner, device_id_type=MESH)
 
     def remote(src, dst, send_sem, recv_sem, device):
         return pltpu.make_async_remote_copy(src_ref=src, dst_ref=dst, send_sem=send_sem, recv_sem=recv_sem, device_id=device, device_id_type=MESH)

time: 216 us -> 216 us (level)
  no operation moved by 1% of the time
where the time goes in v4:
time: 216 us
  Pallas kernels  215 us (100%)
    pallas_call x1, Pallas kernels, run_backward(): pl.pallas_call(backward_kernel, name='backward', out_shape=[pltpu.VMEM((T...  206 us
    pallas_call x1, Pallas kernels, run_backward(): pl.pallas_call(flush_kernel, name='flush', out_shape=[jax.ShapeDtypeStruc...  8.67 us

profile of v4, /device:TPU:0, one launch (start us, length us, event | category | flops | bytes accessed | tf_op | source)
XLA Modules:
  0.0 215.8 jit_solution(5288827495957061011)
XLA Ops:
  0.6 206.3 %backward.1 = (bf16[2048,1536]{1,0:T(8,128)(2,1)S(1)}, f32[2,768,384]{2,1,0:T(8,128)S(1)}, f32[2,768,384]{2,1,0:T(8,128)S(1)}, f32[2,768,384]{2,1,0:T(8,128)S(1)...) custom-call(bf16[2,1536,768]{2,1,0:T(8,128)(2,1)} %wu_hbm.1, ...), custom_call_target="tpu_custom_call" | custom-call | tf_op jit(solution)/shard_map/backward/pallas_call | solution.py:394
  207.0 8.7 %flush.1 = (bf16[1,2048,1536]{2,1,0:T(8,128)(2,1)}, f32[2,1536,768]{2,1,0:T(8,128)}, f32[2,768,1536]{2,1,0:T(8,128)}) custom-call(bf16[2048,1536]{1,0:T(8,128)(2,1)S(1)} %get-tuple-element.12.g, f32[2,768,384]{2,1,0:T(8,128)S(1)} %get-tuple-element.13.refs_0_, f32[2,768,384]{2,1,0:T(8,128)S(1)} %get-tuple-element.14.refs_1_, ...), custom_call_target="tpu_custom_call" | custom-call | tf_op jit(solution)/shard_map/flush/pallas_call | solution.py:425
